TPU v7x, 32 devices: a whole 2x2x4 slice. The times are simulated.
32 devices in a mesh: dp: 32 (over z, y, x, core).
Axes of the slice: x: 2, y: 2, z: 4, core: 2. Of those that a mesh axis runs over, the one named last changes fastest.
Arguments:
- features: bfloat16 [64, 256, 256], P('dp'), may hold values from -6 to 6
- frame_lens: int32 [64], P('dp'), may hold values from 128 to 256
- labels: int32 [64, 48], P('dp'), may hold values from 1 to 255
- label_lens: int32 [64], P('dp'), may hold values from 1 to 48
- w_up: float32 [262144], P('dp'), may hold values from -0.375 to 0.375
- w_down: float32 [262144], P('dp'), may hold values from -0.1875 to 0.1875
- w_out: float32 [65536], P('dp'), may hold values from -1.125 to 1.125
- first_up: float32 [262144], P('dp'), may hold values from -0.00018 to 0.00018
- first_down: float32 [262144], P('dp'), may hold values from -0.00018 to 0.00018
- first_out: float32 [65536], P('dp'), may hold values from -0.00018 to 0.00018
- second_up: float32 [262144], P('dp'), may hold values from 1e-10 to 1e-08
- second_down: float32 [262144], P('dp'), may hold values from 1e-10 to 1e-08
- second_out: float32 [65536], P('dp'), may hold values from 1e-10 to 1e-08
Outputs:
- new_up: float32 [262144], P('dp')
- new_down: float32 [262144], P('dp')
- new_out: float32 [65536], P('dp')
- new_first_up: float32 [262144], P('dp')
- new_first_down: float32 [262144], P('dp')
- new_first_out: float32 [65536], P('dp')
- new_second_up: float32 [262144], P('dp')
- new_second_down: float32 [262144], P('dp')
- new_second_out: float32 [65536], P('dp')
Inputs may be any that keep to these rules, and one draw needn't show every extreme that they name: `labels`: 0 is the blank and is not a label.
All inputs are finite; a program needn't handle non-finite values.
Results may differ from a plain program's by a relative error of at most 0.002.
The roundings to bfloat16 on the way count: a program that leaves them out, or rounds other values in their place, can miss the bound.
Values may be sent and summed in bfloat16 or wider, within the bound.
A program may use at most 64 MiB of HBM per device.

v0:
```python
import math

import jax
import jax.numpy as jnp
from jax import lax
from jax.sharding import PartitionSpec as P

D = 256
FF = 1024
VOCAB = 256
UTT = 2


first_correction = 1.0 - (0.9**10) ** 10
second_correction = 1.0 - (0.999**10) ** 10
negative = -1e30


def log_three(term_one, term_two, term_three):
    largest = jnp.maximum(jnp.maximum(term_one, term_two), term_three)
    return largest + jnp.log(
        jnp.exp(term_one - largest) + jnp.exp(term_two - largest) + jnp.exp(term_three - largest)
    )


def log_total(values, axis):
    largest = jnp.max(values, axis=axis, keepdims=True)
    return jnp.squeeze(largest, axis) + jnp.log(jnp.sum(jnp.exp(values - largest), axis=axis))


def skew_behind(table_in):
    leading = table_in.shape[:-2]
    band_size, states = (table_in.shape[-2], table_in.shape[-1])
    row_length = states + band_size
    padded = jnp.pad(
        table_in, [(0, 0)] * len(leading) + [(0, 0), (band_size, 0)], constant_values=negative
    )
    flattened = padded.reshape(leading + (band_size * row_length,))
    retained = lax.slice_in_dim(
        flattened, band_size, band_size + band_size * (row_length - 1), axis=len(leading)
    )
    return retained.reshape(leading + (band_size, row_length - 1))[..., :states]


def skew_ahead(table_in):
    leading = table_in.shape[:-2]
    band_size, states = (table_in.shape[-2], table_in.shape[-1])
    row_length = states + band_size
    padded = jnp.pad(
        table_in, [(0, 0)] * len(leading) + [(0, 0), (0, band_size)], constant_values=negative
    )
    flattened = padded.reshape(leading + (band_size * row_length,))
    lengthened = jnp.pad(
        flattened, [(0, 0)] * len(leading) + [(0, band_size)], constant_values=negative
    )
    return lengthened.reshape(leading + (band_size, row_length + 1))[..., :states]


def ctc_logit_grad(log_probs, labels, frame_lens, label_lens, loss_scale):
    batch, frames, vocab = log_probs.shape
    label_count = labels.shape[1]
    states = 2 * label_count + 1
    padded_states = (states + 127) // 128 * 128
    frame_block = math.gcd(frames, 1 << (frames.bit_length() - 1) // 2)
    blocks = frames // frame_block
    band_size = 2 * frame_block + 1
    blanks = jnp.zeros_like(labels)
    extended = jnp.concatenate(
        [jnp.stack([blanks, labels], axis=2).reshape(batch, 2 * label_count), blanks[:, :1]], axis=1
    )
    extended = jnp.pad(extended, ((0, 0), (0, padded_states - states)))
    earlier = jnp.concatenate([jnp.full((batch, 2), -1, jnp.int32), extended[:, :-2]], axis=1)
    may_skip = (extended != 0) & (extended != earlier)
    skip_later = jnp.pad(may_skip[:, 2:], ((0, 0), (0, 2)))
    state_ids = jnp.arange(padded_states, dtype=jnp.int32)
    valid_state = state_ids < states
    onehot = (
        (extended[:, :, None] == jnp.arange(vocab, dtype=jnp.int32)[None, None, :])
        & valid_state[None, :, None]
    ).astype(jnp.float32)
    picked = jnp.einsum("btv,bsv->bts", log_probs, onehot, precision=lax.Precision.HIGHEST)
    emitted = jnp.where(valid_state[None, None, :], picked, negative)
    frame_ids = jnp.arange(frames, dtype=jnp.int32)
    alive = frame_ids[None, :] < frame_lens[:, None]
    emit_blocks = emitted.reshape(batch, blocks, frame_block, padded_states).transpose(2, 1, 0, 3)
    alive_blocks = alive.reshape(batch, blocks, frame_block).transpose(2, 1, 0)
    offsets = jnp.arange(band_size, dtype=jnp.int32)
    identity_row = jnp.where(offsets[:, None] == 0, 0.0, negative).astype(jnp.float32)
    identity = jnp.broadcast_to(
        identity_row[None, None, :, :], (blocks, batch, band_size, padded_states)
    )
    skip_grid = may_skip[None, :, None, :]

    def extend_band(transfer, inputs):
        emit_rows, live = inputs
        shifted = jnp.pad(transfer, ((0, 0), (0, 0), (2, 0), (2, 0)), constant_values=negative)
        from_one = shifted[:, :, 1 : band_size + 1, 1 : padded_states + 1]
        from_two = jnp.where(skip_grid, shifted[:, :, :band_size, :padded_states], negative)
        merged = log_three(transfer, from_one, from_two) + emit_rows[:, :, None, :]
        return (jnp.where(live[:, :, None, None], merged, transfer), None)

    transfers, _ = lax.scan(extend_band, identity, (emit_blocks, alive_blocks))
    start = jnp.broadcast_to(
        jnp.where(state_ids == 0, 0.0, negative).astype(jnp.float32)[None, :],
        (batch, padded_states),
    )
    last_state = 2 * label_lens
    at_end = (state_ids[None, :] == last_state[:, None]) | (
        state_ids[None, :] == last_state[:, None] - 1
    )
    finish = jnp.where(at_end, 0.0, negative).astype(jnp.float32)

    def cross_blocks(carry, inputs):
        alpha_in, beta_out = carry
        forward_table, backward_table = inputs
        moved = (
            skew_behind(jnp.broadcast_to(alpha_in[:, None, :], forward_table.shape)) + forward_table
        )
        alpha_next = log_total(moved, 1)
        returned = skew_ahead(backward_table + beta_out[:, None, :])
        beta_prev = log_total(returned, 1)
        return ((alpha_next, beta_prev), (alpha_in, beta_out))

    (alpha_final, _), (alpha_starts, beta_reversed) = lax.scan(
        cross_blocks, (start, finish), (transfers, transfers[::-1])
    )
    beta_ends = beta_reversed[::-1]
    log_total_prob = log_total(alpha_final + finish, 1)

    def inside_block(carry, inputs):
        alpha_now, beta_now = carry
        emit_forward, live_forward, emit_backward, live_backward = inputs
        alpha_pad = jnp.pad(alpha_now, ((0, 0), (0, 0), (2, 0)), constant_values=negative)
        alpha_skip = jnp.where(may_skip[None], alpha_pad[..., :padded_states], negative)
        alpha_new = (
            log_three(alpha_now, alpha_pad[..., 1 : padded_states + 1], alpha_skip) + emit_forward
        )
        alpha_new = jnp.where(live_forward[..., None], alpha_new, alpha_now)
        weighted = beta_now + emit_backward
        weighted_pad = jnp.pad(weighted, ((0, 0), (0, 0), (0, 2)), constant_values=negative)
        beta_skip = jnp.where(skip_later[None], weighted_pad[..., 2 : padded_states + 2], negative)
        beta_new = log_three(weighted, weighted_pad[..., 1 : padded_states + 1], beta_skip)
        beta_new = jnp.where(live_backward[..., None], beta_new, beta_now)
        return ((alpha_new, beta_new), (alpha_new, beta_now))

    _, (alpha_rows, beta_rows) = lax.scan(
        inside_block,
        (alpha_starts, beta_ends),
        (emit_blocks, alive_blocks, emit_blocks[::-1], alive_blocks[::-1]),
    )
    alpha_all = alpha_rows.transpose(2, 1, 0, 3).reshape(batch, frames, padded_states)
    beta_all = beta_rows[::-1].transpose(2, 1, 0, 3).reshape(batch, frames, padded_states)
    occupancy = jnp.exp(alpha_all + beta_all - log_total_prob[:, None, None]) * alive[
        :, :, None
    ].astype(jnp.float32)
    gamma = jnp.einsum("bts,bsv->btv", occupancy, onehot, precision=lax.Precision.HIGHEST)
    probs = jnp.exp(log_probs)
    return loss_scale * (probs * jnp.sum(gamma, axis=-1, keepdims=True) - gamma)


def adam_update(weight, first, second, grad, clip):
    scaled = clip * grad
    new_first = 0.9 * first + 0.1 * scaled
    new_second = 0.999 * second + 0.001 * scaled * scaled
    ratio = new_first / first_correction / (jnp.sqrt(new_second / second_correction) + 1e-08)
    return (weight - 0.001 * ratio, new_first, new_second)


def squares_of(pieces):
    return (
        jnp.sum(pieces[0] * pieces[0])
        + jnp.sum(pieces[1] * pieces[1])
        + jnp.sum(pieces[2] * pieces[2])
    )


def per_device(
    features,
    frame_lens,
    labels,
    label_lens,
    w_up,
    w_down,
    w_out,
    first_up,
    first_down,
    first_out,
    second_up,
    second_down,
    second_out,
):
    devices = lax.axis_size("dp")
    batch, frames, width = features.shape
    full_up, full_down, full_out = (
        lax.all_gather(w_up.astype(jnp.bfloat16), "dp", axis=0, tiled=True),
        lax.all_gather(w_down.astype(jnp.bfloat16), "dp", axis=0, tiled=True),
        lax.all_gather(w_out.astype(jnp.bfloat16), "dp", axis=0, tiled=True),
    )
    up_mat = full_up.reshape(D, FF)
    down_mat = full_down.reshape(FF, D)
    out_mat = full_out.reshape(D, VOCAB)
    loss_scale = 1.0 / (UTT * devices)
    flat_in = features.reshape(batch * frames, width).astype(jnp.float32)
    centre = jnp.mean(flat_in, axis=1, keepdims=True)
    spread = jnp.mean((flat_in - centre) ** 2, axis=1, keepdims=True)
    normalized = ((flat_in - centre) * lax.rsqrt(spread + 1e-05)).astype(jnp.bfloat16)
    activation = jnp.dot(normalized, up_mat, preferred_element_type=jnp.float32)
    hidden = jax.nn.silu(activation).astype(jnp.bfloat16)
    block_out = (
        flat_in + 0.5 * jnp.dot(hidden, down_mat, preferred_element_type=jnp.float32)
    ).astype(jnp.bfloat16)
    logits = jnp.dot(block_out, out_mat, preferred_element_type=jnp.float32)
    log_probs = jax.nn.log_softmax(logits.reshape(batch, frames, VOCAB), axis=-1)
    logit_grad = ctc_logit_grad(log_probs, labels, frame_lens, label_lens, loss_scale)
    logit_grad = logit_grad.reshape(batch * frames, VOCAB).astype(jnp.bfloat16)
    grad_out = jnp.dot(block_out.T, logit_grad, preferred_element_type=jnp.float32).reshape(-1)
    ff_grad = (0.5 * jnp.dot(logit_grad, out_mat.T, preferred_element_type=jnp.float32)).astype(
        jnp.bfloat16
    )
    grad_down = jnp.dot(hidden.T, ff_grad, preferred_element_type=jnp.float32).reshape(-1)
    sigmoid = jax.nn.sigmoid(activation)
    slope = sigmoid * (1.0 + activation * (1.0 - sigmoid))
    act_grad = (jnp.dot(ff_grad, down_mat.T, preferred_element_type=jnp.float32) * slope).astype(
        jnp.bfloat16
    )
    grad_up = jnp.dot(normalized.T, act_grad, preferred_element_type=jnp.float32).reshape(-1)
    summed = lax.psum((grad_up, grad_down, grad_out), "dp")
    total = squares_of(summed)
    place = lax.axis_index("dp")
    share_up = lax.dynamic_slice_in_dim(summed[0], place * w_up.shape[0], w_up.shape[0], 0)
    share_down = lax.dynamic_slice_in_dim(summed[1], place * w_down.shape[0], w_down.shape[0], 0)
    share_out = lax.dynamic_slice_in_dim(summed[2], place * w_out.shape[0], w_out.shape[0], 0)
    clip = 1.0 / jnp.maximum(jnp.sqrt(total), 1.0)
    new_up, new_first_up, new_second_up = adam_update(w_up, first_up, second_up, share_up, clip)
    new_down, new_first_down, new_second_down = adam_update(
        w_down, first_down, second_down, share_down, clip
    )
    new_out, new_first_out, new_second_out = adam_update(
        w_out, first_out, second_out, share_out, clip
    )
    return (
        new_up,
        new_down,
        new_out,
        new_first_up,
        new_first_down,
        new_first_out,
        new_second_up,
        new_second_down,
        new_second_out,
    )


def solution(mesh):
    return jax.shard_map(
        per_device,
        mesh=mesh,
        in_specs=(
            P("dp", None, None),
            P("dp"),
            P("dp", None),
            P("dp"),
            P("dp"),
            P("dp"),
            P("dp"),
            P("dp"),
            P("dp"),
            P("dp"),
            P("dp"),
            P("dp"),
            P("dp"),
        ),
        out_specs=(P("dp"), P("dp"), P("dp"), P("dp"), P("dp"), P("dp"), P("dp"), P("dp"), P("dp")),
        check_vma=False,
    )
```

profile of v0, /device:TPU:0, one launch (start us, length us, event | category | flops | bytes accessed | tf_op | source)
XLA Modules:
  0.0 419.2 jit_solution(9477497240498887268)
XLA Ops:
  9.0 43.6 %all_gather.11 = bf16[65536]{0:T(1024)(128)(2,1)S(1)} all-gather(bf16[2048]{0:T(1024)(128)(2,1)S(1)} %convert_element_type.68), channel_id=1, replica_groups=mesh['dp'=32] {'dp'}, dimensions={0}, use_global_device_ids=true | all-gather | bytes 135168 | tf_op jit(solution)/shard_map/all_gather | solution.py:197
  54.4 1.2 multiply_reduce_fusion.2
  58.1 38.0 %all_gather.9 = bf16[262144]{0:T(1024)(128)(2,1)S(1)} all-gather(bf16[8192]{0:T(1024)(128)(2,1)S(1)} %convert_element_type.64), channel_id=1, replica_groups=mesh['dp'=32] {'dp'}, dimensions={0}, use_global_device_ids=true | all-gather | bytes 540672 | tf_op jit(solution)/shard_map/all_gather | solution.py:195
  96.4 39.5 %all_gather.10 = bf16[262144]{0:T(1024)(128)(2,1)S(1)} all-gather(bf16[8192]{0:T(1024)(128)(2,1)S(1)} %convert_element_type.66), channel_id=1, replica_groups=mesh['dp'=32] {'dp'}, dimensions={0}, use_global_device_ids=true | all-gather | bytes 540672 | tf_op jit(solution)/shard_map/all_gather | solution.py:196
  136.1 2.0 multiply_convert_fusion.1
  142.5 13.3 %while.42 = (s32[]{:T(128)}, f32[16,2,33,128]{3,2,1,0:T(8,128)S(1)}, pred[16,16,2]{1,2,0:T(4,128)(4,1)S(1)}, pred[1,2,1,128]{3,1,2,0:T(4,128)(4,1)S(1)}, f32[16,16,2,128]{3,2,1,0:T(2,128)S(1)}, /*index=5*/s32[]{:T(128)}) while((s32[]{:T(128)}, f32[16,2,33,128]{3,2,1,0:T(8,128)S(1)}, pred[16,16,2]{1,2,0:T(4,128)(4,1)S(1)}, ...), condition=%wide.region_5.6_spmd, body=%wide.region_4.5_spmd.sunk | while | flops 1486850 | bytes 2212333 | solution.py:102
  156.5 16.5 %while.43 = (s32[]{:T(128)}, f32[2,128]{1,0:T(2,128)S(1)}, f32[2,128]{1,0:T(2,128)S(1)}, f32[16,2,128]{2,1,0:T(2,128)S(1)}, f32[16,2,128]{2,1,0:T(2,128)S(1)}, /...) while((s32[]{:T(128)}, f32[2,128]{1,0:T(2,128)S(1)}, ...), condition=%wide.region_11.12_spmd, body=%wide.region_6.11_spmd.sunk | while | flops 75522 | bytes 985053 | solution.py:124
  175.4 82.6 %while.44 = (s32[]{:T(128)}, f32[16,2,128]{2,1,0:T(2,128)S(1)}, f32[16,2,128]{2,1,0:T(2,128)S(1)}, f32[16,16,2,128]{3,0,1,2:T(8,128)}, f32[16,16,2,128]{3,0,1,2:...) while((s32[]{:T(128)}, f32[16,2,128]{2,1,0:T(2,128)S(1)}, ...), condition=%wide.region_13.14_spmd, body=%wide.region_12.13_spmd.sunk | while | flops 90114 | bytes 312273 | solution.py:146
  177.4 1.6 dynamic_update_slice.20
  179.0 1.6 dynamic_update_slice.21
  182.5 1.6 dynamic_update_slice.20
  184.1 1.6 dynamic_update_slice.21
  187.7 1.6 dynamic_update_slice.20
  189.3 1.6 dynamic_update_slice.21
  192.9 1.6 dynamic_update_slice.20
  194.5 1.6 dynamic_update_slice.21
  198.0 1.6 dynamic_update_slice.20
  199.7 1.6 dynamic_update_slice.21
  203.2 1.6 dynamic_update_slice.20
  204.8 1.6 dynamic_update_slice.21
  208.4 1.6 dynamic_update_slice.20
  210.0 1.6 dynamic_update_slice.21
  213.5 1.6 dynamic_update_slice.20
  215.2 1.6 dynamic_update_slice.21
  218.7 1.6 dynamic_update_slice.20
  220.3 1.6 dynamic_update_slice.21
  223.8 1.6 dynamic_update_slice.20
  225.5 1.6 dynamic_update_slice.21
  229.0 1.6 dynamic_update_slice.20
  230.6 1.6 dynamic_update_slice.21
  234.2 1.6 dynamic_update_slice.20
  235.8 1.6 dynamic_update_slice.21
  239.3 1.6 dynamic_update_slice.20
  240.9 1.6 dynamic_update_slice.21
  244.5 1.6 dynamic_update_slice.20
  246.1 1.6 dynamic_update_slice.21
  249.6 1.6 dynamic_update_slice.20
  251.2 1.6 dynamic_update_slice.21
  254.8 1.6 dynamic_update_slice.20
  256.4 1.6 dynamic_update_slice.21
  263.4 1.5 copy.56
  265.1 2.8 convolution_bitcast_fusion.1
  269.2 132.9 %all-reduce.14.cloned.1.call-done = (f32[262144]{0:T(1024)}, f32[262144]{0:T(1024)}, f32[65536]{0:T(1024)}) async-done(((f32[262144]{0:T(1024)}, f32[262144]{0:T(1024)}, f32[65536]{0:T(1024)}), (f32[262144]{0:T(1024)}, f32[262144]{0:T(1024)}, f32[65536]{0:T(1024)})) %all-reduce.14.cloned.1.call-update) | async-done | bytes 2359312 | tf_op jit(solution)/shard_map/psum | solution.py:227
  402.1 1.6 multiply_reduce_fusion.3
  403.7 2.4 multiply_reduce_fusion
  408.2 1.4 multiply_subtract_fusion
  409.6 1.4 multiply_subtract_fusion.1
  411.1 1.3 multiply_subtract_fusion.2
  (580 shorter events, 78.7 us)
Async XLA Ops:
  7.2 89.2 %copy-start.3 = (f32[8192]{0:T(1024)S(1)}, f32[8192]{0:T(1024)}, u32[]{:S(2)}) copy-start(f32[8192]{0:T(1024)} %param.24) | copy-start | bytes 98308
  7.2 394.9 %all-reduce.14.cloned.1.call-start = ((), (), s32[]{:S(2)}) async-start(), calls=%async_computation | async-start | bytes 4718592 | tf_op jit(solution)/shard_map/psum | solution.py:227
  7.2 132.3 %copy-start.17 = (pred[128]{0:T(512)(128)(4,1)}, pred[128]{0:T(512)(128)(4,1)S(1)}, u32[]{:S(2)}) copy-start(pred[128]{0:T(512)(128)(4,1)S(1)} %iota_compare_fusion.1) | copy-start | bytes 388
  136.0 2.0 copy-start
  138.1 1.0 copy-start.1
  138.1 2.2 copy-start.16
  142.5 13.4 %copy-start.19 = (s32[2]{0:T(128)S(1)}, s32[2]{0:T(128)}, u32[]{:S(2)}) copy-start(s32[2]{0:T(128)} %param.22) | copy-start | bytes 28
  155.9 0.5 copy-start.14
  155.9 0.6 copy-start.15
  173.0 87.1 %copy-start.18 = (pred[128]{0:T(512)(128)(4,1)S(1)}, pred[128]{0:T(512)(128)(4,1)}, u32[]{:S(2)}) copy-start(pred[128]{0:T(512)(128)(4,1)} %copy-done.17) | copy-start | bytes 388
  260.1 2.8 copy-start.2
  262.9 2.0 copy-start.13
  262.9 2.0 copy-start.12
  269.1 139.1 %copy-start.5 = (f32[8192]{0:T(1024)S(1)}, f32[8192]{0:T(1024)}, u32[]{:S(2)}) copy-start(f32[8192]{0:T(1024)} %param.27) | copy-start | bytes 98308
  269.1 139.1 %copy-start.6 = (f32[8192]{0:T(1024)S(1)}, f32[8192]{0:T(1024)}, u32[]{:S(2)}) copy-start(f32[8192]{0:T(1024)} %param.30) | copy-start | bytes 98308
  269.1 140.5 %copy-start.4 = (f32[8192]{0:T(1024)S(1)}, f32[8192]{0:T(1024)}, u32[]{:S(2)}) copy-start(f32[8192]{0:T(1024)} %param.23) | copy-start | bytes 98308
  269.1 140.5 %copy-start.7 = (f32[8192]{0:T(1024)S(1)}, f32[8192]{0:T(1024)}, u32[]{:S(2)}) copy-start(f32[8192]{0:T(1024)} %param.26) | copy-start | bytes 98308
  269.1 140.5 %copy-start.8 = (f32[8192]{0:T(1024)S(1)}, f32[8192]{0:T(1024)}, u32[]{:S(2)}) copy-start(f32[8192]{0:T(1024)} %param.29) | copy-start | bytes 98308
  269.1 141.9 %copy-start.9 = (f32[2048]{0:T(1024)S(1)}, f32[2048]{0:T(1024)}, u32[]{:S(2)}) copy-start(f32[2048]{0:T(1024)} %param.25) | copy-start | bytes 24580
  269.1 141.9 %copy-start.10 = (f32[2048]{0:T(1024)S(1)}, f32[2048]{0:T(1024)}, u32[]{:S(2)}) copy-start(f32[2048]{0:T(1024)} %param.28) | copy-start | bytes 24580
  269.1 141.9 %copy-start.11 = (f32[2048]{0:T(1024)S(1)}, f32[2048]{0:T(1024)}, u32[]{:S(2)}) copy-start(f32[2048]{0:T(1024)} %param.31) | copy-start | bytes 24580
Sparse Core Ops, SparseCore 0:
  269.3 132.7 all-reduce.13
where the time goes:
time: 422 us; the launch traced here: 419 us
  waiting for transfers between devices  133 us (32%)
  blocking collectives  121 us (29%)
  local copies, waits for them, and re-layouts  91.4 us (22%)
  other arithmetic  47 us (11%)
  between operations  16.5 us (4%)
  matrix products  7.62 us (2%)
    psum x1, waiting for transfers between devices, per_device(): summed = lax.psum((grad_up, grad_down, grad_out), 'dp')  133 us
    dynamic_update_slice x64, local copies, waits for them, and re-layouts, ctc_logit_grad(): lax.scan(inside_block, (alpha_starts, beta_ends), (emit_blocks, alive_blo...  52.2 us
    all_gather x1, blocking collectives, per_device(): lax.all_gather(w_out.astype(jnp.bfloat16), 'dp', axis=0, tiled=True)  43.6 us
    all_gather x1, blocking collectives, per_device(): lax.all_gather(w_down.astype(jnp.bfloat16), 'dp', axis=0, tiled=True)  39.5 us
    all_gather x1, blocking collectives, per_device(): lax.all_gather(w_up.astype(jnp.bfloat16), 'dp', axis=0, tiled=True)  38 us
    add x16, other arithmetic, inside_block(): weighted = beta_now + emit_backward  13.6 us
    broadcast_in_dim x32, local copies, waits for them, and re-layouts, inside_block(): beta_new = jnp.where(live_backward[..., None], beta_new, beta_now)  12.2 us
    select_n x16, other arithmetic, extend_band(): return (jnp.where(live[:, :, None, None], merged, transfer), None)  10.1 us
  transfers between devices with their start and end apart: 1, of which 1 were waited for; matrix products, arithmetic and copies ran while one was open for 0% of the time, Pallas kernels for 0%

commit v1 on v0

v1 whole, which is shorter than its diff:
```python
import functools

import jax
import jax.numpy as jnp
from jax import lax
from jax.experimental import pallas as pl
from jax.experimental.pallas import tpu as pltpu
from jax.sharding import PartitionSpec as P

D = 256
FF = 1024
VOCAB = 256
LANES = 128
MESH = pl.DeviceIdType.MESH

first_correction = 1.0 - (0.9**10) ** 10
second_correction = 1.0 - (0.999**10) ** 10
negative = -1e30
VMEM = pl.BlockSpec(memory_space=pltpu.VMEM)
SMEM = pl.BlockSpec(memory_space=pltpu.SMEM)


def flip(me, bit):
    return me + bit - 2 * bit * ((me // bit) % 2)


def bit_orders(devices):
    bits = [1 << k for k in range(devices.bit_length() - 1)]
    core, rest = bits[:1], bits[1:]
    down = rest[::-1]
    swapped = down[:-2] + down[-2:][::-1]
    turned = down[-2:] + down[:-2]
    return (down + core, swapped + core, turned + core)


def subsets(bits):
    offsets = [0]
    for bit in bits:
        offsets = offsets + [offset + bit for offset in offsets]
    return offsets


def place_with(me, free, pattern):
    place = me
    for bit in free:
        if pattern & bit:
            place = flip(place, bit)
    return place


def gather_kernel(devices, w_up, w_down, w_out, full_up, full_down, full_out, send_sem, recv_sem):
    me = lax.axis_index("dp")
    orders = bit_orders(devices)
    barrier = pltpu.get_barrier_semaphore()
    for bit in orders[0]:
        pl.semaphore_signal(barrier, inc=1, device_id=(flip(me, bit),), device_id_type=MESH)
    fulls = (full_up, full_down, full_out)
    for shard, full in zip((w_up, w_down, w_out), fulls):
        rows, width = full.shape[1:]
        parts = width // LANES
        for part in range(parts):
            full[me, :, part * LANES : (part + 1) * LANES] = shard[
                pl.ds(part, rows, stride=parts), :
            ].astype(jnp.bfloat16)
    pl.semaphore_wait(barrier, len(orders[0]))

    copies = [{}, {}, {}]

    def send(which, pattern, stage):
        order, full = orders[which], fulls[which]
        owner = place_with(me, order[:stage], pattern)
        slot = pattern + order[stage]
        copy = pltpu.make_async_remote_copy(
            src_ref=full.at[owner],
            dst_ref=full.at[owner],
            send_sem=send_sem.at[which, slot],
            recv_sem=recv_sem.at[which, slot],
            device_id=(flip(me, order[stage]),),
            device_id_type=MESH,
        )
        copy.start()
        copies[which][slot] = copy

    steps = len(orders[0])
    for which in range(3):
        for stage in range(steps):
            send(which, 0, stage)
    for stage in range(steps):
        for pattern_at in range(1 << stage):
            for which in range(3):
                order = orders[which]
                pattern = subsets(order[:stage])[pattern_at] + order[stage]
                copies[which][pattern].wait_recv()
                for later in range(stage + 1, steps):
                    send(which, pattern, later)
    for which in range(3):
        for copy in copies[which].values():
            copy.wait_send()


def gather_weights(devices, w_up, w_down, w_out):
    shapes = []
    for shard, width in ((w_up, FF), (w_down, D), (w_out, VOCAB)):
        shapes.append(
            jax.ShapeDtypeStruct((devices, shard.size // width, width), jnp.bfloat16)
        )
    return pl.pallas_call(
        functools.partial(gather_kernel, devices),
        out_shape=shapes,
        in_specs=[VMEM] * 3,
        out_specs=[VMEM] * 3,
        scratch_shapes=[
            pltpu.SemaphoreType.DMA((3, devices)),
            pltpu.SemaphoreType.DMA((3, devices)),
        ],
        compiler_params=pltpu.CompilerParams(collective_id=0, has_side_effects=True),
        name="gather_weights",
    )(w_up, w_down, w_out)


def dot_rows(left, right):
    return jnp.dot(left, right, preferred_element_type=jnp.float32)


def dot_last(left, right, precision=None):
    return lax.dot_general(
        left, right, (((1,), (1,)), ((), ())), precision=precision,
        preferred_element_type=jnp.float32,
    )


def dot_first(left, right):
    return lax.dot_general(
        left, right, (((0,), (0,)), ((), ())), preferred_element_type=jnp.float32
    )


def step_kernel(
    loss_scale,
    frame_lens,
    label_lens,
    features,
    labels,
    up_mat,
    down_mat,
    out_mat,
    grad_up,
    grad_down,
    grad_out,
    normalized,
    activation,
    hidden,
    block_out,
    log_probs,
    emitted,
    alpha_rows,
    beta_rows,
    logit_grad,
    ff_grad,
    act_grad,
):
    utterances, label_count = labels.shape
    total = features.shape[0]
    frames = total // utterances
    states = 2 * label_count + 1
    block = min(128, total)

    @pl.loop(0, total // block)
    def _(step):
        rows = pl.ds(pl.multiple_of(step * block, block), block)
        flat_in = features[rows, :].astype(jnp.float32)
        centre = jnp.mean(flat_in, axis=1, keepdims=True)
        shifted = flat_in - centre
        spread = jnp.mean(shifted * shifted, axis=1, keepdims=True)
        norm = (shifted * lax.rsqrt(spread + 1e-05)).astype(jnp.bfloat16)
        normalized[rows, :] = norm
        act = dot_rows(norm, up_mat[...])
        activation[rows, :] = act
        hid = (act * (1.0 / (1.0 + jnp.exp(-act)))).astype(jnp.bfloat16)
        hidden[rows, :] = hid
        out_rows = (flat_in + 0.5 * dot_rows(hid, down_mat[...])).astype(jnp.bfloat16)
        block_out[rows, :] = out_rows
        logits = dot_rows(out_rows, out_mat[...])
        top = jnp.max(logits, axis=1, keepdims=True)
        low = logits - top
        log_probs[rows, :] = low - jnp.log(jnp.sum(jnp.exp(low), axis=1, keepdims=True))

    label_ids = lax.broadcasted_iota(jnp.int32, (label_count, LANES), 0)
    state_at = lax.broadcasted_iota(jnp.int32, (label_count, LANES), 1)
    spread_now = (state_at == 2 * label_ids + 1).astype(jnp.bfloat16)
    spread_back = (state_at == 2 * label_ids + 3).astype(jnp.bfloat16)
    spread_ahead = (state_at == 2 * label_ids - 1).astype(jnp.bfloat16)
    label_rows = jnp.concatenate(
        [
            labels[...].astype(jnp.float32),
            jnp.zeros((8 - utterances, label_count), jnp.float32),
        ],
        axis=0,
    ).astype(jnp.bfloat16)
    extended = dot_rows(label_rows, spread_now)
    earlier = dot_rows(label_rows, spread_back)
    later = dot_rows(label_rows, spread_ahead)
    row_ids = lax.broadcasted_iota(jnp.int32, (8, LANES), 0)
    lane_ids = lax.broadcasted_iota(jnp.int32, (8, LANES), 1)
    may_skip = (extended > 0.5) & (extended != earlier)
    skip_later = (later > 0.5) & (later != extended)
    skip_add = jnp.where(may_skip, 0.0, negative)
    later_add = jnp.where(skip_later, 0.0, negative)
    start = jnp.where(lane_ids < 2, 0.0, negative)
    ends = jnp.full((8, LANES), -9, jnp.int32)
    first_frame = jnp.full((8, LANES), -9, jnp.int32)
    for utterance in range(utterances):
        ends = jnp.where(row_ids == utterance, 2 * label_lens[utterance], ends)
        first_frame = jnp.where(row_ids == utterance, frame_lens[utterance] - 1, first_frame)
    finish = jnp.where((lane_ids == ends) | (lane_ids == ends - 1), 0.0, negative)

    emitted[...] = jnp.full(emitted.shape, negative, jnp.float32)
    vocab_ids = lax.broadcasted_iota(jnp.int32, (VOCAB, LANES), 0).astype(jnp.float32)
    lanes_wide = lax.broadcasted_iota(jnp.int32, (VOCAB, LANES), 1)
    frame_lanes = lax.broadcasted_iota(jnp.int32, (frames, LANES), 1)
    onehots = []
    for utterance in range(utterances):
        onehot = jnp.where(
            (vocab_ids == extended[utterance : utterance + 1, :]) & (lanes_wide < states), 1.0, 0.0
        )
        onehots.append(onehot)
        picked = jnp.dot(
            log_probs[utterance * frames : (utterance + 1) * frames, :],
            onehot,
            precision=lax.Precision.HIGHEST,
            preferred_element_type=jnp.float32,
        )
        emitted[:, utterance, :] = jnp.where(frame_lanes < states, picked, negative)

    def log_three(one, two, three):
        top = jnp.maximum(jnp.maximum(one, two), three)
        return top + jnp.log(jnp.exp(one - top) + jnp.exp(two - top) + jnp.exp(three - top))

    def advance(frame, carry):
        alpha, weighted = carry
        back = frames - 1 - frame
        base = log_three(
            alpha, pltpu.roll(alpha, 1, 1), pltpu.roll(alpha, 2, 1) + skip_add
        )
        base = jnp.where(jnp.full((8, LANES), frame, jnp.int32) == 0, start, base)
        other = log_three(
            weighted,
            pltpu.roll(weighted, LANES - 1, 1),
            pltpu.roll(weighted, LANES - 2, 1) + later_add,
        )
        other = jnp.where(first_frame == back, finish, other)
        alpha_rows[frame] = base
        beta_rows[back] = other
        return (base + emitted[frame], other + emitted[back])

    nothing = jnp.full((8, LANES), negative, jnp.float32)
    lax.fori_loop(0, frames, advance, (nothing, nothing), unroll=8)

    frame_ids = lax.broadcasted_iota(jnp.int32, (frames, LANES), 0)
    for utterance in range(utterances):
        joint = (
            alpha_rows[:, utterance, :] + emitted[:, utterance, :] + beta_rows[:, utterance, :]
        )
        top = jnp.max(joint, axis=1, keepdims=True)
        mass = jnp.exp(joint - top)
        share = mass / jnp.sum(mass, axis=1, keepdims=True)
        occupancy = jnp.where(frame_ids < frame_lens[utterance], share, 0.0)
        gamma = dot_last(occupancy, onehots[utterance], lax.Precision.HIGHEST)
        rows = slice(utterance * frames, (utterance + 1) * frames)
        probs = jnp.exp(log_probs[rows, :])
        held = jnp.sum(occupancy, axis=1, keepdims=True)
        logit_grad[rows, :] = (loss_scale * (probs * held - gamma)).astype(jnp.bfloat16)

    @pl.loop(0, total // block)
    def _(step):
        rows = pl.ds(pl.multiple_of(step * block, block), block)
        grad_rows = (0.5 * dot_last(logit_grad[rows, :], out_mat[...])).astype(jnp.bfloat16)
        ff_grad[rows, :] = grad_rows
        act = activation[rows, :]
        sigmoid = 1.0 / (1.0 + jnp.exp(-act))
        slope = sigmoid * (1.0 + act * (1.0 - sigmoid))
        act_grad[rows, :] = (dot_last(grad_rows, down_mat[...]) * slope).astype(jnp.bfloat16)

    grad_up[...] = dot_first(normalized[...], act_grad[...])
    grad_down[...] = dot_first(hidden[...], ff_grad[...])
    grad_out[...] = dot_first(block_out[...], logit_grad[...])


def local_step(loss_scale, frame_lens, label_lens, features, labels, up_mat, down_mat, out_mat):
    total = features.shape[0]
    frames = total // labels.shape[0]
    return pl.pallas_call(
        functools.partial(step_kernel, loss_scale),
        out_shape=[
            jax.ShapeDtypeStruct((D, FF), jnp.float32),
            jax.ShapeDtypeStruct((FF, D), jnp.float32),
            jax.ShapeDtypeStruct((D, VOCAB), jnp.float32),
        ],
        in_specs=[SMEM, SMEM] + [VMEM] * 5,
        out_specs=[VMEM] * 3,
        scratch_shapes=[
            pltpu.VMEM((total, D), jnp.bfloat16),
            pltpu.VMEM((total, FF), jnp.float32),
            pltpu.VMEM((total, FF), jnp.bfloat16),
            pltpu.VMEM((total, D), jnp.bfloat16),
            pltpu.VMEM((total, VOCAB), jnp.float32),
            pltpu.VMEM((frames, 8, LANES), jnp.float32),
            pltpu.VMEM((frames, 8, LANES), jnp.float32),
            pltpu.VMEM((frames, 8, LANES), jnp.float32),
            pltpu.VMEM((total, VOCAB), jnp.bfloat16),
            pltpu.VMEM((total, D), jnp.bfloat16),
            pltpu.VMEM((total, FF), jnp.bfloat16),
        ],
        compiler_params=pltpu.CompilerParams(vmem_limit_bytes=40 << 20),
        name="local_step",
    )(frame_lens, label_lens, features, labels, up_mat, down_mat, out_mat)


def sum_kernel(devices, *refs):
    grads, reduced, squares = refs[:3], refs[3:6], refs[6]
    received, staged = refs[7:10], refs[10:13]
    own_squares, send_sem, recv_sem, small_send, small_recv = refs[13:]
    me = lax.axis_index("dp")
    orders = [order[::-1] for order in bit_orders(devices)]
    steps = len(orders[0])
    barrier = pltpu.get_barrier_semaphore()

    @pl.loop(1, devices)
    def _(shift):
        pl.semaphore_signal(
            barrier, inc=1, device_id=((me + shift) % devices,), device_id_type=MESH
        )

    pl.semaphore_wait(barrier, devices - 1)

    copies = [{}, {}, {}]

    def sum_of(which, place, pattern, stage):
        value = grads[which][place]
        order = orders[which]
        for past in range(stage):
            slot = pattern + order[past]
            copies[which][slot].wait_recv()
            value = value + received[which][slot]
        return value

    for stage in range(steps):
        for at in range(1 << (steps - 1 - stage)):
            for which in range(3):
                order = orders[which]
                rest = order[stage + 1 :]
                pattern = subsets(rest[::-1])[::-1][at] + order[stage]
                place = place_with(me, order, pattern)
                landing = pattern - order[stage]
                if stage == 0:
                    source = grads[which].at[place]
                else:
                    staged[which][pattern] = sum_of(which, place, pattern, stage)
                    source = staged[which].at[pattern]
                slot = landing + order[stage]
                copy = pltpu.make_async_remote_copy(
                    src_ref=source,
                    dst_ref=received[which].at[slot],
                    send_sem=send_sem.at[which, slot],
                    recv_sem=recv_sem.at[which, slot],
                    device_id=(flip(me, order[stage]),),
                    device_id_type=MESH,
                )
                copy.start()
                copies[which][slot] = copy

    own = jnp.zeros((1, LANES), jnp.float32)
    for which in range(3):
        value = sum_of(which, me, 0, steps)
        rows, width = value.shape
        parts = width // LANES
        for part in range(parts):
            piece = value[:, part * LANES : (part + 1) * LANES]
            reduced[which][pl.ds(part, rows, stride=parts), :] = piece
            own = own + jnp.sum(piece * piece, axis=0, keepdims=True)
    own_squares[...] = own
    squares[0] = own

    def small_copy(shift):
        return pltpu.make_async_remote_copy(
            src_ref=own_squares,
            dst_ref=squares.at[shift],
            send_sem=small_send.at[shift],
            recv_sem=small_recv.at[shift],
            device_id=((me + shift) % devices,),
            device_id_type=MESH,
        )

    @pl.loop(1, devices)
    def _(shift):
        small_copy(shift).start()

    for which in range(3):
        for copy in copies[which].values():
            copy.wait_send()

    @pl.loop(1, devices)
    def _(shift):
        small_copy(shift).wait()


def sum_gradients(devices, grads):
    blocks = [grad.reshape(devices, grad.shape[0] // devices, grad.shape[1]) for grad in grads]
    shapes = [
        jax.ShapeDtypeStruct((block[0].size // LANES, LANES), jnp.float32) for block in blocks
    ]
    buffers = [pltpu.VMEM(block.shape, jnp.float32) for block in blocks]
    return pl.pallas_call(
        functools.partial(sum_kernel, devices),
        out_shape=shapes + [jax.ShapeDtypeStruct((devices, 1, LANES), jnp.float32)],
        in_specs=[VMEM] * 3,
        out_specs=[VMEM] * 4,
        scratch_shapes=buffers
        + buffers
        + [
            pltpu.VMEM((1, LANES), jnp.float32),
            pltpu.SemaphoreType.DMA((3, devices)),
            pltpu.SemaphoreType.DMA((3, devices)),
            pltpu.SemaphoreType.DMA((devices,)),
            pltpu.SemaphoreType.DMA((devices,)),
        ],
        compiler_params=pltpu.CompilerParams(
            collective_id=1, has_side_effects=True, vmem_limit_bytes=50 << 20
        ),
        name="sum_gradients",
    )(*blocks)


def adam_kernel(squares, *refs):
    weights, firsts, seconds, grads, outs = (refs[at : at + 3] for at in (0, 3, 6, 9, 12))
    new_firsts, new_seconds = refs[15:18], refs[18:21]
    total = jnp.sum(squares[...])
    clip = 1.0 / jnp.maximum(jnp.sqrt(jnp.full((1, LANES), total)), 1.0)
    for which in range(3):
        scaled = clip * grads[which][...]
        first = 0.9 * firsts[which][...] + 0.1 * scaled
        second = 0.999 * seconds[which][...] + 0.001 * scaled * scaled
        ratio = first / first_correction / (jnp.sqrt(second / second_correction) + 1e-08)
        outs[which][...] = weights[which][...] - 0.001 * ratio
        new_firsts[which][...] = first
        new_seconds[which][...] = second


def adam(squares, weights, firsts, seconds, grads):
    shapes = [jax.ShapeDtypeStruct(weight.shape, jnp.float32) for weight in weights]
    return pl.pallas_call(
        adam_kernel,
        out_shape=shapes * 3,
        in_specs=[VMEM] * 13,
        out_specs=[VMEM] * 9,
        name="adam",
    )(squares, *weights, *firsts, *seconds, *grads)


def per_device(
    features,
    frame_lens,
    labels,
    label_lens,
    w_up,
    w_down,
    w_out,
    first_up,
    first_down,
    first_out,
    second_up,
    second_down,
    second_out,
):
    devices = lax.axis_size("dp")
    batch, frames, width = features.shape

    def lined(*arrays):
        return [array.reshape(array.shape[0] // LANES, LANES) for array in arrays]

    weights = lined(w_up, w_down, w_out)
    full_up, full_down, full_out = gather_weights(devices, *weights)
    grads = local_step(
        1.0 / (batch * devices),
        frame_lens,
        label_lens,
        features.reshape(batch * frames, width),
        labels,
        full_up.reshape(D, FF),
        full_down.reshape(FF, D),
        full_out.reshape(D, VOCAB),
    )
    *shares, squares = sum_gradients(devices, grads)
    results = adam(
        squares,
        weights,
        lined(first_up, first_down, first_out),
        lined(second_up, second_down, second_out),
        shares,
    )
    return tuple(result.reshape(-1) for result in results)


def solution(mesh):
    flat = P("dp")
    return jax.shard_map(
        per_device,
        mesh=mesh,
        in_specs=(P("dp", None, None), flat, P("dp", None), flat) + (flat,) * 9,
        out_specs=(flat,) * 9,
        check_vma=False,
    )
```

time: 422 us -> 90.8 us (0.22)
  waiting for transfers between devices: 133 us -> 0 us
  blocking collectives: 121 us -> 0 us
  local copies, waits for them, and re-layouts: 91.4 us -> 7.01 us
  Pallas kernels: 0 us -> 82.7 us
  other arithmetic: 47 us -> 0 us
  between operations: 16.5 us -> 0.7 us
  matrix products: 7.62 us -> 0 us
    psum x1 -> x0, waiting for transfers between devices: 133 us -> none  [per_device(): summed = lax.psum((grad_up, grad_down, grad_out), 'dp')]
    all_gather x3 -> x0, blocking collectives: 121 us -> none  [the longest x1 43.6 us: per_device(): lax.all_gather(w_out.astype(jnp.bfloat16), 'dp', axis=0, tiled=True)]
    pallas_call x0 -> x4, Pallas kernels: none -> 82.7 us  [the longest x1 31.8 us: local_step(): pl.pallas_call(functools.partial(step_kernel, loss_scale), out_shape=[jax...]
    dynamic_update_slice x80 -> x0, local copies, waits for them, and re-layouts: 52.4 us -> none  [the longest x64 52.2 us: ctc_logit_grad(): lax.scan(inside_block, (alpha_starts, beta_ends), (emit_blocks, alive_blo...]
    broadcast_in_dim x114 -> x0, local copies, waits for them, and re-layouts: 15.8 us -> none  [the longest x32 12.2 us: inside_block(): beta_new = jnp.where(live_backward[..., None], beta_new, beta_now)]
    add x66 -> x0, other arithmetic: 15.4 us -> none  [the longest x16 13.6 us: inside_block(): weighted = beta_now + emit_backward]
    select_n x35 -> x0, other arithmetic: 12.7 us -> none  [the longest x16 10.1 us: extend_band(): return (jnp.where(live[:, :, None, None], merged, transfer), None)]
    reshape x70 -> x0, local copies, waits for them, and re-layouts: 9.9 us -> none  [the longest x16 2.63 us: skew_behind(): flattened = padded.reshape(leading + (band_size * row_length,))]
  transfers between devices with their start and end apart: 1 -> 0, of which waited for: 1 -> 0; matrix products, arithmetic and copies ran while one was open for 0% -> 0% of each run, Pallas kernels for 0% -> 0%
where the time goes in v1:
time: 90.8 us; the launch traced here: 90.4 us
  Pallas kernels  82.7 us (91%)
  local copies, waits for them, and re-layouts  7.01 us (8%)
    pallas_call x1, Pallas kernels, local_step(): pl.pallas_call(functools.partial(step_kernel, loss_scale), out_shape=[jax...  31.8 us
    pallas_call x1, Pallas kernels, sum_gradients(): pl.pallas_call(functools.partial(sum_kernel, devices), out_shape=shapes +...  27.4 us
    pallas_call x1, Pallas kernels, gather_weights(): pl.pallas_call(functools.partial(gather_kernel, devices), out_shape=shape...  21.7 us
    unnamed x22, local copies, waits for them, and re-layouts  7.01 us

profile of v1, /device:TPU:0, one launch (start us, length us, event | category | flops | bytes accessed | tf_op | source)
XLA Modules:
  0.0 90.4 jit_solution(4504322938887393575)
XLA Ops:
  0.6 21.7 %gather_weights.1 = (bf16[32,8,1024]{2,1,0:T(8,128)(2,1)}, bf16[32,32,256]{2,1,0:T(8,128)(2,1)}, bf16[32,8,256]{2,1,0:T(8,128)(2,1)}) custom-call(f32[64,128]{1,0:T(8,128)} %bitcast.32, f32[64,128]{1,0:T(8,128)} %bitcast.34, f32[16,128]{1,0:T(8,128)} %bitcast.40), custom_call_target="tpu_custom_call" | custom-call | tf_op jit(solution)/shard_map/gather_weights/pallas_call | solution.py:107
  22.3 0.0 copy-start.10
  22.3 0.0 copy-start.8
  22.3 0.0 copy-start.9
  22.3 0.6 copy-done.10
  23.0 0.0 copy-done.8
  23.0 0.0 copy-done.9
  23.0 0.0 copy-start
  23.0 1.0 %copy-done = bf16[32,8,1024]{2,1,0:T(8,128)(2,1)S(1)} copy-done((bf16[32,8,1024]{2,1,0:T(8,128)(2,1)S(1)}, bf16[32,8,1024]{2,1,0:T(8,128)(2,1)}, u32[]{:S(2)}) %copy-start) | copy-done | bytes 524312
  24.0 0.0 copy-start.1
  24.0 1.0 %copy-done.1 = bf16[32,32,256]{2,1,0:T(8,128)(2,1)S(1)} copy-done((bf16[32,32,256]{2,1,0:T(8,128)(2,1)S(1)}, bf16[32,32,256]{2,1,0:T(8,128)(2,1)}, u32[]{:S(2)}) %copy-start.1) | copy-done | bytes 524312
  25.1 0.0 copy-start.2
  25.1 0.9 %copy-done.2 = bf16[2,256,256]{2,1,0:T(8,128)(2,1)S(1)} copy-done((bf16[2,256,256]{2,1,0:T(8,128)(2,1)S(1)}, bf16[2,256,256]{2,1,0:T(8,128)(2,1)}, u32[]{:S(2)}) %copy-start.2) | copy-done | bytes 262168
  26.0 0.0 copy-start.3
  26.0 0.9 copy-done.3
  26.9 31.8 %local_step.1 = (f32[256,1024]{1,0:T(8,128)S(1)}, f32[1024,256]{1,0:T(8,128)S(1)}, f32[256,256]{1,0:T(8,128)S(1)}) custom-call(s32[2]{0:T(128)S(1)} %copy-done.9, s32[2]{0:T(128)S(1)} %copy-done.10, bf16[512,256]{1,0:T(8,128)(2,1)S(1)} %bitcast.30, s32[2,48]{1,0:T(2,128)S(1)} %copy-done.8, bf16[256,1024]{1,0:T(8,128)(2,1)S(1)} %bitcast.27, ...), custom_call_target="tpu_custom_call" | custom-call | tf_op jit(solution)/shard_map/local_step/pallas_call | solution.py:292
  58.7 27.4 %sum_gradients.1 = (f32[64,128]{1,0:T(8,128)S(1)}, f32[64,128]{1,0:T(8,128)S(1)}, f32[16,128]{1,0:T(8,128)S(1)}, f32[32,1,128]{2,1,0:T(1,128)S(1)}) custom-call(f32[32,8,1024]{2,1,0:T(8,128)S(1)} %bitcast.25, f32[32,32,256]{2,1,0:T(8,128)S(1)} %bitcast.26, f32[32,8,256]{2,1,0:T(8,128)S(1)} %bitcast.29), custom_call_target="tpu_custom_call" | custom-call | tf_op jit(solution)/shard_map/sum_gradients/pallas_call | solution.py:413
  86.2 0.0 copy-start.4
  86.2 0.6 copy-done.4
  86.8 0.0 copy-start.5
  86.8 0.6 copy-done.5
  87.4 0.0 copy-start.6
  87.4 0.6 copy-done.6
  88.0 0.0 copy-start.7
  88.0 0.6 copy-done.7
  88.6 1.8 %adam.1 = (f32[64,128]{1,0:T(8,128)}, f32[64,128]{1,0:T(8,128)}, f32[16,128]{1,0:T(8,128)}, f32[64,128]{1,0:T(8,128)}, f32[64,128]{1,0:T(8,128)}, /*index=5*/f32...) custom-call(f32[32,1,128]{2,1,0:T(1,128)} %copy-done.6, f32[64,128]{1,0:T(8,128)} %bitcast.33, ...), custom_call_target="tpu_custom_call" | custom-call | tf_op jit(solution)/shard_map/adam/pallas_call | solution.py:451
Async XLA Ops:
  22.3 0.7 copy-start.10
  22.3 0.7 copy-start.8
  22.3 0.7 copy-start.9
  23.0 1.0 %copy-start = (bf16[32,8,1024]{2,1,0:T(8,128)(2,1)S(1)}, bf16[32,8,1024]{2,1,0:T(8,128)(2,1)}, u32[]{:S(2)}) copy-start(bf16[32,8,1024]{2,1,0:T(8,128)(2,1)} %get-tuple-element.28) | copy-start | bytes 1572868
  24.0 1.0 %copy-start.1 = (bf16[32,32,256]{2,1,0:T(8,128)(2,1)S(1)}, bf16[32,32,256]{2,1,0:T(8,128)(2,1)}, u32[]{:S(2)}) copy-start(bf16[32,32,256]{2,1,0:T(8,128)(2,1)} %get-tuple-element.29) | copy-start | bytes 1572868
  25.1 0.9 %copy-start.2 = (bf16[2,256,256]{2,1,0:T(8,128)(2,1)S(1)}, bf16[2,256,256]{2,1,0:T(8,128)(2,1)}, u32[]{:S(2)}) copy-start(bf16[2,256,256]{2,1,0:T(8,128)(2,1)} %param.13) | copy-start | bytes 786436
  26.0 0.9 %copy-start.3 = (bf16[32,8,256]{2,1,0:T(8,128)(2,1)S(1)}, bf16[32,8,256]{2,1,0:T(8,128)(2,1)}, u32[]{:S(2)}) copy-start(bf16[32,8,256]{2,1,0:T(8,128)(2,1)} %get-tuple-element.30) | copy-start | bytes 393220
  86.2 0.6 copy-start.4
  86.8 0.6 copy-start.5
  87.4 0.6 copy-start.6
  88.0 0.6 copy-start.7

commit v2 on v1

v2 whole, which is shorter than its diff:
```python
import functools

import jax
import jax.numpy as jnp
from jax import lax
from jax.experimental import pallas as pl
from jax.experimental.pallas import tpu as pltpu
from jax.sharding import PartitionSpec as P

D = 256
FF = 1024
VOCAB = 256
LANES = 128
MESH = pl.DeviceIdType.MESH

first_correction = 1.0 - (0.9**10) ** 10
second_correction = 1.0 - (0.999**10) ** 10
negative = -1e30
VMEM = pl.BlockSpec(memory_space=pltpu.VMEM)
SMEM = pl.BlockSpec(memory_space=pltpu.SMEM)


def flip(me, bit):
    return me + bit - 2 * bit * ((me // bit) % 2)


def bit_orders(devices):
    bits = [1 << k for k in range(devices.bit_length() - 1)]
    core, rest = bits[:1], bits[1:]
    down = rest[::-1]
    swapped = down[:-2] + down[-2:][::-1]
    turned = down[-2:] + down[:-2]
    return (down + core, swapped + core, turned + core)


def subsets(bits):
    offsets = [0]
    for bit in bits:
        offsets = offsets + [offset + bit for offset in offsets]
    return offsets


def place_with(me, free, pattern):
    place = me
    for bit in free:
        if pattern & bit:
            place = flip(place, bit)
    return place


class Gather:
    def __init__(self, me, devices, fulls, send_sem, recv_sem):
        self.me, self.fulls = me, fulls
        self.send_sem, self.recv_sem = send_sem, recv_sem
        self.orders = bit_orders(devices)
        self.steps = len(self.orders[0])
        self.copies = [{}, {}, {}]

    def fill(self, shards):
        for shard, full in zip(shards, self.fulls):
            rows, width = full.shape[1:]
            parts = width // LANES
            for part in range(parts):
                full[self.me, :, part * LANES : (part + 1) * LANES] = shard[
                    pl.ds(part, rows, stride=parts), :
                ].astype(jnp.bfloat16)

    def send(self, which, pattern, stage):
        order, full = self.orders[which], self.fulls[which]
        owner = place_with(self.me, order[:stage], pattern)
        slot = pattern + order[stage]
        copy = pltpu.make_async_remote_copy(
            src_ref=full.at[owner],
            dst_ref=full.at[owner],
            send_sem=self.send_sem.at[which, slot],
            recv_sem=self.recv_sem.at[which, slot],
            device_id=(flip(self.me, order[stage]),),
            device_id_type=MESH,
        )
        copy.start()
        self.copies[which][slot] = copy

    def pass_on(self):
        for which in range(3):
            for stage in range(self.steps):
                self.send(which, 0, stage)
        for stage in range(self.steps - 1):
            for at in range(1 << stage):
                for which in range(3):
                    order = self.orders[which]
                    pattern = subsets(order[:stage])[at] + order[stage]
                    self.copies[which][pattern].wait_recv()
                    for later in range(stage + 1, self.steps):
                        self.send(which, pattern, later)

    def arrive(self, which):
        order = self.orders[which]
        for pattern in subsets(order[:-1]):
            self.copies[which][pattern + order[-1]].wait_recv()

    def close(self):
        for copies in self.copies:
            for copy in copies.values():
                copy.wait_send()


def greet(me, devices, barrier):
    @pl.loop(1, devices)
    def _(shift):
        pl.semaphore_signal(
            barrier, inc=1, device_id=((me + shift) % devices,), device_id_type=MESH
        )


def gather_kernel(devices, w_up, w_down, w_out, full_up, full_down, full_out, send_sem, recv_sem):
    me = lax.axis_index("dp")
    barrier = pltpu.get_barrier_semaphore()
    greet(me, devices, barrier)
    gather = Gather(me, devices, (full_up, full_down, full_out), send_sem, recv_sem)
    gather.fill((w_up, w_down, w_out))
    pl.semaphore_wait(barrier, devices - 1)
    gather.pass_on()
    for which in range(3):
        gather.arrive(which)
    gather.close()


def gather_weights(devices, w_up, w_down, w_out):
    shapes = []
    for shard, width in ((w_up, FF), (w_down, D), (w_out, VOCAB)):
        shapes.append(
            jax.ShapeDtypeStruct((devices, shard.size // width, width), jnp.bfloat16)
        )
    return pl.pallas_call(
        functools.partial(gather_kernel, devices),
        out_shape=shapes,
        in_specs=[VMEM] * 3,
        out_specs=[VMEM] * 3,
        scratch_shapes=[
            pltpu.SemaphoreType.DMA((3, devices)),
            pltpu.SemaphoreType.DMA((3, devices)),
        ],
        compiler_params=pltpu.CompilerParams(collective_id=0, has_side_effects=True),
        name="gather_weights",
    )(w_up, w_down, w_out)


def dot_rows(left, right):
    return jnp.dot(left, right, preferred_element_type=jnp.float32)


def dot_last(left, right, precision=None):
    return lax.dot_general(
        left, right, (((1,), (1,)), ((), ())), precision=precision,
        preferred_element_type=jnp.float32,
    )


def dot_first(left, right):
    return lax.dot_general(
        left, right, (((0,), (0,)), ((), ())), preferred_element_type=jnp.float32
    )


def row_blocks(total, body):
    block = min(128, total)

    @pl.loop(0, total // block)
    def _(step):
        body(pl.ds(pl.multiple_of(step * block, block), block))


def normalize(features, normalized):
    def body(rows):
        flat_in = features[rows, :].astype(jnp.float32)
        centre = jnp.mean(flat_in, axis=1, keepdims=True)
        shifted = flat_in - centre
        spread = jnp.mean(shifted * shifted, axis=1, keepdims=True)
        normalized[rows, :] = (shifted * lax.rsqrt(spread + 1e-05)).astype(jnp.bfloat16)

    row_blocks(features.shape[0], body)


def project_up(normalized, up_mat, activation, hidden):
    def body(rows):
        act = dot_rows(normalized[rows, :], up_mat[...].reshape(D, FF))
        activation[rows, :] = act
        hidden[rows, :] = (act * (1.0 / (1.0 + jnp.exp(-act)))).astype(jnp.bfloat16)

    row_blocks(normalized.shape[0], body)


def project_down(features, hidden, down_mat, out_mat, block_out, log_probs):
    def body(rows):
        flat_in = features[rows, :].astype(jnp.float32)
        out_rows = (flat_in + 0.5 * dot_rows(hidden[rows, :], down_mat[...].reshape(FF, D))).astype(
            jnp.bfloat16
        )
        block_out[rows, :] = out_rows
        logits = dot_rows(out_rows, out_mat[...].reshape(D, VOCAB))
        top = jnp.max(logits, axis=1, keepdims=True)
        low = logits - top
        log_probs[rows, :] = low - jnp.log(jnp.sum(jnp.exp(low), axis=1, keepdims=True))

    row_blocks(features.shape[0], body)


def ctc_grad(
    loss_scale,
    frame_lens,
    label_lens,
    labels,
    log_probs,
    emitted,
    alpha_rows,
    beta_rows,
    logit_grad,
):
    utterances, label_count = labels.shape
    frames = log_probs.shape[0] // utterances
    states = 2 * label_count + 1

    label_ids = lax.broadcasted_iota(jnp.int32, (label_count, LANES), 0)
    state_at = lax.broadcasted_iota(jnp.int32, (label_count, LANES), 1)
    spread_now = (state_at == 2 * label_ids + 1).astype(jnp.bfloat16)
    spread_back = (state_at == 2 * label_ids + 3).astype(jnp.bfloat16)
    spread_ahead = (state_at == 2 * label_ids - 1).astype(jnp.bfloat16)
    label_rows = jnp.concatenate(
        [
            labels[...].astype(jnp.float32),
            jnp.zeros((8 - utterances, label_count), jnp.float32),
        ],
        axis=0,
    ).astype(jnp.bfloat16)
    extended = dot_rows(label_rows, spread_now)
    earlier = dot_rows(label_rows, spread_back)
    later = dot_rows(label_rows, spread_ahead)
    row_ids = lax.broadcasted_iota(jnp.int32, (8, LANES), 0)
    lane_ids = lax.broadcasted_iota(jnp.int32, (8, LANES), 1)
    may_skip = (extended > 0.5) & (extended != earlier)
    skip_later = (later > 0.5) & (later != extended)
    skip_add = jnp.where(may_skip, 0.0, negative)
    later_add = jnp.where(skip_later, 0.0, negative)
    ends = jnp.full((8, LANES), -9, jnp.int32)
    first_frame = jnp.full((8, LANES), -9, jnp.int32)
    for utterance in range(utterances):
        ends = jnp.where(row_ids == utterance, 2 * label_lens[utterance], ends)
        first_frame = jnp.where(row_ids == utterance, frame_lens[utterance] - 1, first_frame)
    finish = jnp.where((lane_ids == ends) | (lane_ids == ends - 1), 0.0, negative)

    emitted[...] = jnp.full(emitted.shape, negative, jnp.float32)
    vocab_ids = lax.broadcasted_iota(jnp.int32, (VOCAB, LANES), 0).astype(jnp.float32)
    lanes_wide = lax.broadcasted_iota(jnp.int32, (VOCAB, LANES), 1)
    frame_lanes = lax.broadcasted_iota(jnp.int32, (frames, LANES), 1)
    onehots = []
    for utterance in range(utterances):
        onehot = jnp.where(
            (vocab_ids == extended[utterance : utterance + 1, :]) & (lanes_wide < states), 1.0, 0.0
        )
        onehots.append(onehot)
        picked = jnp.dot(
            log_probs[utterance * frames : (utterance + 1) * frames, :],
            onehot,
            precision=lax.Precision.HIGHEST,
            preferred_element_type=jnp.float32,
        )
        emitted[:, utterance, :] = jnp.where(frame_lanes < states, picked, negative)

    def log_three(one, two, three):
        top = jnp.maximum(jnp.maximum(one, two), three)
        return top + jnp.log(jnp.exp(one - top) + jnp.exp(two - top) + jnp.exp(three - top))

    def ahead(values, count):
        return pltpu.roll(values, count, 1) if count else values

    def behind(values, count):
        return pltpu.roll(values, LANES - count, 1) if count else values

    skips = [ahead(skip_add, count) for count in range(3)]
    later_skips = [behind(later_add, count) for count in range(3)]
    finishes = [behind(finish, count) for count in range(3)]

    def advance(pair, carry):
        alpha, weighted = carry
        frame = 2 * pair
        back = frames - 1 - frame
        moved = [ahead(alpha, count) for count in range(5)]
        other = [behind(weighted, count) for count in range(5)]
        emit, emit_back = emitted[frame], emitted[back]
        ends_here = first_frame == back
        firsts, lasts = [], []
        for count in range(3):
            base = log_three(moved[count], moved[count + 1], moved[count + 2] + skips[count])
            rest = log_three(other[count], other[count + 1], other[count + 2] + later_skips[count])
            rest = jnp.where(ends_here, finishes[count], rest)
            if count == 0:
                alpha_rows[frame] = base
                beta_rows[back] = rest
            firsts.append(base + ahead(emit, count))
            lasts.append(rest + behind(emit_back, count))
        base = log_three(firsts[0], firsts[1], firsts[2] + skips[0])
        rest = log_three(lasts[0], lasts[1], lasts[2] + later_skips[0])
        rest = jnp.where(first_frame == back - 1, finish, rest)
        alpha_rows[frame + 1] = base
        beta_rows[back - 1] = rest
        return (base + emitted[frame + 1], rest + emitted[back - 1])

    nothing = jnp.full((8, LANES), negative, jnp.float32)
    start = jnp.where(lane_ids == 0, 0.0, negative)
    lax.fori_loop(0, frames // 2, advance, (start, nothing), unroll=4)

    frame_ids = lax.broadcasted_iota(jnp.int32, (frames, LANES), 0)
    for utterance in range(utterances):
        joint = (
            alpha_rows[:, utterance, :] + emitted[:, utterance, :] + beta_rows[:, utterance, :]
        )
        top = jnp.max(joint, axis=1, keepdims=True)
        mass = jnp.exp(joint - top)
        share = mass / jnp.sum(mass, axis=1, keepdims=True)
        occupancy = jnp.where(frame_ids < frame_lens[utterance], share, 0.0)
        gamma = dot_last(occupancy, onehots[utterance], lax.Precision.HIGHEST)
        rows = slice(utterance * frames, (utterance + 1) * frames)
        probs = jnp.exp(log_probs[rows, :])
        held = jnp.sum(occupancy, axis=1, keepdims=True)
        logit_grad[rows, :] = (loss_scale * (probs * held - gamma)).astype(jnp.bfloat16)


def grad_ff(logit_grad, out_mat, ff_grad):
    def body(rows):
        ff_grad[rows, :] = (
            0.5 * dot_last(logit_grad[rows, :], out_mat[...].reshape(D, VOCAB))
        ).astype(jnp.bfloat16)

    row_blocks(logit_grad.shape[0], body)


def grad_act(ff_grad, down_mat, activation, act_grad):
    def body(rows):
        act = activation[rows, :]
        sigmoid = 1.0 / (1.0 + jnp.exp(-act))
        slope = sigmoid * (1.0 + act * (1.0 - sigmoid))
        act_grad[rows, :] = (
            dot_last(ff_grad[rows, :], down_mat[...].reshape(FF, D)) * slope
        ).astype(jnp.bfloat16)

    row_blocks(ff_grad.shape[0], body)


def step_kernel(
    loss_scale,
    frame_lens,
    label_lens,
    features,
    labels,
    up_mat,
    down_mat,
    out_mat,
    grad_up,
    grad_down,
    grad_out,
    normalized,
    activation,
    hidden,
    block_out,
    log_probs,
    emitted,
    alpha_rows,
    beta_rows,
    logit_grad,
    ff_grad,
    act_grad,
):
    normalize(features, normalized)
    project_up(normalized, up_mat, activation, hidden)
    project_down(features, hidden, down_mat, out_mat, block_out, log_probs)
    ctc_grad(
        loss_scale, frame_lens, label_lens, labels, log_probs, emitted, alpha_rows, beta_rows,
        logit_grad,
    )
    grad_ff(logit_grad, out_mat, ff_grad)
    grad_act(ff_grad, down_mat, activation, act_grad)
    grad_up[...] = dot_first(normalized[...], act_grad[...])
    grad_down[...] = dot_first(hidden[...], ff_grad[...])
    grad_out[...] = dot_first(block_out[...], logit_grad[...])


def step_scratch(total, frames):
    return [
        pltpu.VMEM((total, D), jnp.bfloat16),
        pltpu.VMEM((total, FF), jnp.float32),
        pltpu.VMEM((total, FF), jnp.bfloat16),
        pltpu.VMEM((total, D), jnp.bfloat16),
        pltpu.VMEM((total, VOCAB), jnp.float32),
        pltpu.VMEM((frames, 8, LANES), jnp.float32),
        pltpu.VMEM((frames, 8, LANES), jnp.float32),
        pltpu.VMEM((frames, 8, LANES), jnp.float32),
        pltpu.VMEM((total, VOCAB), jnp.bfloat16),
        pltpu.VMEM((total, D), jnp.bfloat16),
        pltpu.VMEM((total, FF), jnp.bfloat16),
    ]


def local_step(loss_scale, frame_lens, label_lens, features, labels, up_mat, down_mat, out_mat):
    total = features.shape[0]
    frames = total // labels.shape[0]
    return pl.pallas_call(
        functools.partial(step_kernel, loss_scale),
        out_shape=[
            jax.ShapeDtypeStruct((D, FF), jnp.float32),
            jax.ShapeDtypeStruct((FF, D), jnp.float32),
            jax.ShapeDtypeStruct((D, VOCAB), jnp.float32),
        ],
        in_specs=[SMEM, SMEM] + [VMEM] * 5,
        out_specs=[VMEM] * 3,
        scratch_shapes=step_scratch(total, frames),
        compiler_params=pltpu.CompilerParams(vmem_limit_bytes=40 << 20),
        name="local_step",
    )(frame_lens, label_lens, features, labels, up_mat, down_mat, out_mat)


class Sum:
    def __init__(self, me, devices, grads, received, staged, send_sem, recv_sem):
        self.me, self.grads, self.received, self.staged = me, grads, received, staged
        self.send_sem, self.recv_sem = send_sem, recv_sem
        self.orders = [order[::-1] for order in bit_orders(devices)]
        self.steps = len(self.orders[0])
        self.copies = [{}, {}, {}]

    def sum_of(self, which, place, pattern, stage):
        value = self.grads[which][place]
        for bit in self.orders[which][:stage]:
            self.copies[which][pattern + bit].wait_recv()
            value = value + self.received[which][pattern + bit]
        return value

    def send(self, which, stage):
        order = self.orders[which]
        for offset in subsets(order[stage + 1 :][::-1])[::-1]:
            slot = offset + order[stage]
            place = place_with(self.me, order, slot)
            if stage == 0:
                source = self.grads[which].at[place]
            else:
                self.staged[which][slot] = self.sum_of(which, place, slot, stage)
                source = self.staged[which].at[slot]
            copy = pltpu.make_async_remote_copy(
                src_ref=source,
                dst_ref=self.received[which].at[slot],
                send_sem=self.send_sem.at[which, slot],
                recv_sem=self.recv_sem.at[which, slot],
                device_id=(flip(self.me, order[stage]),),
                device_id_type=MESH,
            )
            copy.start()
            self.copies[which][slot] = copy

    def finish(self, devices, reduced, squares, own_squares, small_send, small_recv):
        me = self.me
        own = jnp.zeros((1, LANES), jnp.float32)
        for which in (2, 1, 0):
            value = self.sum_of(which, me, 0, self.steps)
            rows, width = value.shape
            parts = width // LANES
            for part in range(parts):
                piece = value[:, part * LANES : (part + 1) * LANES]
                reduced[which][pl.ds(part, rows, stride=parts), :] = piece
                own = own + jnp.sum(piece * piece, axis=0, keepdims=True)
        own_squares[...] = own
        squares[0] = own

        def small_copy(shift):
            return pltpu.make_async_remote_copy(
                src_ref=own_squares,
                dst_ref=squares.at[shift],
                send_sem=small_send.at[shift],
                recv_sem=small_recv.at[shift],
                device_id=((me + shift) % devices,),
                device_id_type=MESH,
            )

        @pl.loop(1, devices)
        def _(shift):
            small_copy(shift).start()

        for copies in self.copies:
            for copy in copies.values():
                copy.wait_send()

        @pl.loop(1, devices)
        def _(shift):
            small_copy(shift).wait()


def sum_kernel(devices, *refs):
    grads, reduced, squares = refs[:3], refs[3:6], refs[6]
    received, staged = refs[7:10], refs[10:13]
    own_squares, send_sem, recv_sem, small_send, small_recv = refs[13:]
    me = lax.axis_index("dp")
    barrier = pltpu.get_barrier_semaphore()
    greet(me, devices, barrier)
    pl.semaphore_wait(barrier, devices - 1)
    total = Sum(me, devices, grads, received, staged, send_sem, recv_sem)
    for stage in range(total.steps):
        for which in range(3):
            total.send(which, stage)
    total.finish(devices, reduced, squares, own_squares, small_send, small_recv)


def fused_kernel(devices, loss_scale, *refs):
    frame_lens, label_lens, features, labels = refs[:4]
    shards, reduced, squares = refs[4:7], refs[7:10], refs[10]
    fulls, grads, received, staged = refs[11:14], refs[14:17], refs[17:20], refs[20:23]
    gather_send, gather_recv, own_squares, send_sem, recv_sem, small_send, small_recv = refs[23:30]
    normalized, activation, hidden, block_out, log_probs = refs[30:35]
    emitted, alpha_rows, beta_rows, logit_grad, ff_grad, act_grad = refs[35:]
    up_mat, down_mat, out_mat = fulls
    me = lax.axis_index("dp")
    barrier = pltpu.get_barrier_semaphore()
    greet(me, devices, barrier)
    gather = Gather(me, devices, fulls, gather_send, gather_recv)
    gather.fill(shards)
    normalize(features, normalized)
    pl.semaphore_wait(barrier, devices - 1)
    gather.pass_on()
    gather.arrive(0)
    project_up(normalized, up_mat, activation, hidden)
    gather.arrive(1)
    gather.arrive(2)
    project_down(features, hidden, down_mat, out_mat, block_out, log_probs)
    ctc_grad(
        loss_scale, frame_lens, label_lens, labels, log_probs, emitted, alpha_rows, beta_rows,
        logit_grad,
    )
    total = Sum(me, devices, grads, received, staged, send_sem, recv_sem)
    pending = [list(range(total.steps)) for _ in range(3)]

    def advance(*whiches):
        for which in whiches:
            if pending[which]:
                total.send(which, pending[which].pop(0))

    def put(which, value):
        grads[which][...] = value.reshape(grads[which].shape)

    grad_ff(logit_grad, out_mat, ff_grad)
    put(1, dot_first(hidden[...], ff_grad[...]))
    advance(1)
    grad_act(ff_grad, down_mat, activation, act_grad)
    advance(1)
    put(0, dot_first(normalized[...], act_grad[...]))
    advance(0)
    put(2, dot_first(block_out[...], logit_grad[...]))
    advance(2)
    while any(pending):
        advance(1, 0, 2)
    total.finish(devices, reduced, squares, own_squares, small_send, small_recv)
    gather.close()


def fused_step(loss_scale, devices, frame_lens, label_lens, features, labels, weights):
    total = features.shape[0]
    frames = total // labels.shape[0]
    blocks = [
        (devices, weight.size // width, width)
        for weight, width in zip(weights, (FF, D, VOCAB))
    ]
    wide = [pltpu.VMEM(block, jnp.float32) for block in blocks]
    return pl.pallas_call(
        functools.partial(fused_kernel, devices, loss_scale),
        out_shape=[jax.ShapeDtypeStruct(weight.shape, jnp.float32) for weight in weights]
        + [jax.ShapeDtypeStruct((devices, 1, LANES), jnp.float32)],
        in_specs=[SMEM, SMEM] + [VMEM] * 5,
        out_specs=[VMEM] * 4,
        scratch_shapes=[pltpu.VMEM(block, jnp.bfloat16) for block in blocks]
        + wide * 3
        + [
            pltpu.SemaphoreType.DMA((3, devices)),
            pltpu.SemaphoreType.DMA((3, devices)),
            pltpu.VMEM((1, LANES), jnp.float32),
            pltpu.SemaphoreType.DMA((3, devices)),
            pltpu.SemaphoreType.DMA((3, devices)),
            pltpu.SemaphoreType.DMA((devices,)),
            pltpu.SemaphoreType.DMA((devices,)),
        ]
        + step_scratch(total, frames),
        compiler_params=pltpu.CompilerParams(
            collective_id=2, has_side_effects=True, vmem_limit_bytes=40 << 20
        ),
        name="fused_step",
    )(frame_lens, label_lens, features, labels, *weights)


def sum_gradients(devices, grads):
    blocks = [grad.reshape(devices, grad.shape[0] // devices, grad.shape[1]) for grad in grads]
    shapes = [
        jax.ShapeDtypeStruct((block[0].size // LANES, LANES), jnp.float32) for block in blocks
    ]
    buffers = [pltpu.VMEM(block.shape, jnp.float32) for block in blocks]
    return pl.pallas_call(
        functools.partial(sum_kernel, devices),
        out_shape=shapes + [jax.ShapeDtypeStruct((devices, 1, LANES), jnp.float32)],
        in_specs=[VMEM] * 3,
        out_specs=[VMEM] * 4,
        scratch_shapes=buffers
        + buffers
        + [
            pltpu.VMEM((1, LANES), jnp.float32),
            pltpu.SemaphoreType.DMA((3, devices)),
            pltpu.SemaphoreType.DMA((3, devices)),
            pltpu.SemaphoreType.DMA((devices,)),
            pltpu.SemaphoreType.DMA((devices,)),
        ],
        compiler_params=pltpu.CompilerParams(
            collective_id=1, has_side_effects=True, vmem_limit_bytes=50 << 20
        ),
        name="sum_gradients",
    )(*blocks)


def adam_kernel(squares, *refs):
    weights, firsts, seconds, grads, outs = (refs[at : at + 3] for at in (0, 3, 6, 9, 12))
    new_firsts, new_seconds = refs[15:18], refs[18:21]
    total = jnp.sum(squares[...])
    clip = 1.0 / jnp.maximum(jnp.sqrt(jnp.full((1, LANES), total)), 1.0)
    for which in range(3):
        scaled = clip * grads[which][...]
        first = 0.9 * firsts[which][...] + 0.1 * scaled
        second = 0.999 * seconds[which][...] + 0.001 * scaled * scaled
        ratio = first / first_correction / (jnp.sqrt(second / second_correction) + 1e-08)
        outs[which][...] = weights[which][...] - 0.001 * ratio
        new_firsts[which][...] = first
        new_seconds[which][...] = second


def adam(squares, weights, firsts, seconds, grads):
    shapes = [jax.ShapeDtypeStruct(weight.shape, jnp.float32) for weight in weights]
    return pl.pallas_call(
        adam_kernel,
        out_shape=shapes * 3,
        in_specs=[VMEM] * 13,
        out_specs=[VMEM] * 9,
        compiler_params=pltpu.CompilerParams(vmem_limit_bytes=8 << 20),
        name="adam",
    )(squares, *weights, *firsts, *seconds, *grads)


def per_device(
    features,
    frame_lens,
    labels,
    label_lens,
    w_up,
    w_down,
    w_out,
    first_up,
    first_down,
    first_out,
    second_up,
    second_down,
    second_out,
):
    devices = lax.axis_size("dp")
    batch, frames, width = features.shape

    def lined(*arrays):
        return [array.reshape(array.shape[0] // LANES, LANES) for array in arrays]

    weights = lined(w_up, w_down, w_out)
    loss_scale = 1.0 / (batch * devices)
    rows_in = features.reshape(batch * frames, width)
    if w_up.size % (8 * FF) == 0 and w_out.size % (8 * VOCAB) == 0:
        *shares, squares = fused_step(
            loss_scale, devices, frame_lens, label_lens, rows_in, labels, weights
        )
    else:
        full_up, full_down, full_out = gather_weights(devices, *weights)
        grads = local_step(
            loss_scale,
            frame_lens,
            label_lens,
            rows_in,
            labels,
            full_up.reshape(D, FF),
            full_down.reshape(FF, D),
            full_out.reshape(D, VOCAB),
        )
        *shares, squares = sum_gradients(devices, grads)
    results = adam(
        squares,
        weights,
        lined(first_up, first_down, first_out),
        lined(second_up, second_down, second_out),
        shares,
    )
    return tuple(result.reshape(-1) for result in results)


def solution(mesh):
    flat = P("dp")
    return jax.shard_map(
        per_device,
        mesh=mesh,
        in_specs=(P("dp", None, None), flat, P("dp", None), flat) + (flat,) * 9,
        out_specs=(flat,) * 9,
        check_vma=False,
    )
```

time: 90.8 us -> 77.3 us (0.85)
  Pallas kernels: 82.7 us -> 73.1 us
  local copies, waits for them, and re-layouts: 7.01 us -> 3.17 us
    pallas_call x3 -> x1, Pallas kernels: 80.9 us -> 72.2 us  [fused_step(): pl.pallas_call(functools.partial(fused_kernel, devices, loss_scale), out_...]
    unnamed x22 -> x26, local copies, waits for them, and re-layouts: 7.01 us -> 3.17 us
    pallas_call x1, Pallas kernels: 1.79 us -> 0.87 us  [adam(): pl.pallas_call(adam_kernel, out_shape=shapes * 3, in_specs=[VMEM] * 13, o...]
where the time goes in v2:
time: 77.3 us; the launch traced here: 77 us
  Pallas kernels  73.1 us (95%)
  local copies, waits for them, and re-layouts  3.17 us (4%)
    pallas_call x1, Pallas kernels, fused_step(): pl.pallas_call(functools.partial(fused_kernel, devices, loss_scale), out_...  72.2 us
    unnamed x26, local copies, waits for them, and re-layouts  3.17 us

profile of v2, /device:TPU:0, one launch (start us, length us, event | category | flops | bytes accessed | tf_op | source)
XLA Modules:
  0.0 77.0 jit_solution(12559425844375287620)
XLA Ops:
  0.6 0.0 copy-start.7
  0.7 0.0 copy-start.12
  0.7 0.0 copy-start.10
  0.7 0.0 copy-start.11
  0.7 0.7 copy-done.7
  1.3 0.0 copy-done.12
  1.3 0.0 copy-done.10
  1.4 0.0 copy-done.11
  1.4 0.0 copy-start
  1.4 0.9 %copy-done = bf16[2,256,256]{2,1,0:T(8,128)(2,1)S(1)} copy-done((bf16[2,256,256]{2,1,0:T(8,128)(2,1)S(1)}, bf16[2,256,256]{2,1,0:T(8,128)(2,1)}, u32[]{:S(2)}) %copy-start) | copy-done | bytes 262168
  2.3 0.0 copy-start.1
  2.3 0.8 copy-done.1
  3.1 0.0 copy-start.2
  3.1 0.8 copy-done.2
  3.8 0.0 copy-start.3
  3.8 0.0 copy-start.4
  3.8 0.0 copy-start.5
  3.8 0.0 copy-start.6
  3.8 0.0 copy-start.8
  3.9 0.0 copy-start.9
  3.9 72.2 %fused_step.1 = (f32[64,128]{1,0:T(8,128)S(1)}, f32[64,128]{1,0:T(8,128)S(1)}, f32[16,128]{1,0:T(8,128)S(1)}, f32[32,1,128]{2,1,0:T(1,128)S(1)}) custom-call(s32[2]{0:T(128)S(1)} %copy-done.11, s32[2]{0:T(128)S(1)} %copy-done.12, bf16[512,256]{1,0:T(8,128)(2,1)S(1)} %bitcast.19, s32[2,48]{1,0:T(2,128)S(1)} %copy-done.10, f32[64,128]{1,0:T(8,128)S(1)} %bitcast.20, ...), custom_call_target="tpu_custom_call" | custom-call | tf_op jit(solution)/shard_map/fused_step/pallas_call | solution.py:568
  76.0 0.0 copy-done.3
  76.1 0.0 copy-done.4
  76.1 0.0 copy-done.5
  76.1 0.0 copy-done.6
  76.1 0.0 copy-done.8
  76.1 0.0 copy-done.9
  76.1 0.9 %adam.1 = (f32[64,128]{1,0:T(8,128)}, f32[64,128]{1,0:T(8,128)}, f32[16,128]{1,0:T(8,128)}, f32[64,128]{1,0:T(8,128)}, f32[64,128]{1,0:T(8,128)}, /*index=5*/f32...) custom-call(f32[32,1,128]{2,1,0:T(1,128)S(1)} %get-tuple-element.22.squares, ...), custom_call_target="tpu_custom_call" | custom-call | tf_op jit(solution)/shard_map/adam/pallas_call | solution.py:637
Async XLA Ops:
  0.6 0.7 copy-start.7
  0.7 0.7 copy-start.12
  0.7 0.7 copy-start.10
  0.7 0.7 copy-start.11
  1.4 1.0 %copy-start = (bf16[2,256,256]{2,1,0:T(8,128)(2,1)S(1)}, bf16[2,256,256]{2,1,0:T(8,128)(2,1)}, u32[]{:S(2)}) copy-start(bf16[2,256,256]{2,1,0:T(8,128)(2,1)} %param.13) | copy-start | bytes 786436
  2.3 0.8 copy-start.1
  3.1 0.8 copy-start.2
  3.8 72.2 %copy-start.3 = (f32[8192]{0:T(1024)S(1)}, f32[8192]{0:T(1024)}, u32[]{:S(2)}) copy-start(f32[8192]{0:T(1024)} %param.20) | copy-start | bytes 98308
  3.8 72.2 %copy-start.4 = (f32[8192]{0:T(1024)S(1)}, f32[8192]{0:T(1024)}, u32[]{:S(2)}) copy-start(f32[8192]{0:T(1024)} %param.21) | copy-start | bytes 98308
  3.8 72.2 %copy-start.5 = (f32[8192]{0:T(1024)S(1)}, f32[8192]{0:T(1024)}, u32[]{:S(2)}) copy-start(f32[8192]{0:T(1024)} %param.23) | copy-start | bytes 98308
  3.8 72.2 %copy-start.6 = (f32[8192]{0:T(1024)S(1)}, f32[8192]{0:T(1024)}, u32[]{:S(2)}) copy-start(f32[8192]{0:T(1024)} %param.24) | copy-start | bytes 98308
  3.8 72.2 %copy-start.8 = (f32[2048]{0:T(1024)S(1)}, f32[2048]{0:T(1024)}, u32[]{:S(2)}) copy-start(f32[2048]{0:T(1024)} %param.22) | copy-start | bytes 24580
  3.9 72.2 %copy-start.9 = (f32[2048]{0:T(1024)S(1)}, f32[2048]{0:T(1024)}, u32[]{:S(2)}) copy-start(f32[2048]{0:T(1024)} %param.25) | copy-start | bytes 24580

commit v3 on v2

--- a/solution.py
+++ b/solution.py
@@ -18,6 +18,7 @@
 negative = -1e30
 VMEM = pl.BlockSpec(memory_space=pltpu.VMEM)
 SMEM = pl.BlockSpec(memory_space=pltpu.SMEM)
+HBM = pl.BlockSpec(memory_space=pltpu.HBM)
 
 
 def flip(me, bit):
@@ -307,7 +308,7 @@
 
     nothing = jnp.full((8, LANES), negative, jnp.float32)
     start = jnp.where(lane_ids == 0, 0.0, negative)
-    lax.fori_loop(0, frames // 2, advance, (start, nothing), unroll=4)
+    lax.fori_loop(0, frames // 2, advance, (start, nothing), unroll=8)
 
     frame_ids = lax.broadcasted_iota(jnp.int32, (frames, LANES), 0)
     for utterance in range(utterances):
@@ -512,13 +513,24 @@
     fulls, grads, received, staged = refs[11:14], refs[14:17], refs[17:20], refs[20:23]
     gather_send, gather_recv, own_squares, send_sem, recv_sem, small_send, small_recv = refs[23:30]
     normalized, activation, hidden, block_out, log_probs = refs[30:35]
-    emitted, alpha_rows, beta_rows, logit_grad, ff_grad, act_grad = refs[35:]
+    emitted, alpha_rows, beta_rows, logit_grad, ff_grad, act_grad = refs[35:41]
+    held, load_sem = refs[41:45], refs[45]
     up_mat, down_mat, out_mat = fulls
     me = lax.axis_index("dp")
+    loads = [
+        pltpu.make_async_copy(source, target, load_sem.at[at])
+        for at, (source, target) in enumerate(zip((*shards, features), held))
+    ]
+    for load in loads:
+        load.start()
+    shards, features = held[:3], held[3]
     barrier = pltpu.get_barrier_semaphore()
     greet(me, devices, barrier)
     gather = Gather(me, devices, fulls, gather_send, gather_recv)
+    for load in loads[:3]:
+        load.wait()
     gather.fill(shards)
+    loads[3].wait()
     normalize(features, normalized)
     pl.semaphore_wait(barrier, devices - 1)
     gather.pass_on()
@@ -569,7 +581,7 @@
         functools.partial(fused_kernel, devices, loss_scale),
         out_shape=[jax.ShapeDtypeStruct(weight.shape, jnp.float32) for weight in weights]
         + [jax.ShapeDtypeStruct((devices, 1, LANES), jnp.float32)],
-        in_specs=[SMEM, SMEM] + [VMEM] * 5,
+        in_specs=[SMEM, SMEM, HBM, VMEM] + [HBM] * 3,
         out_specs=[VMEM] * 4,
         scratch_shapes=[pltpu.VMEM(block, jnp.bfloat16) for block in blocks]
         + wide * 3
@@ -582,9 +594,11 @@
             pltpu.SemaphoreType.DMA((devices,)),
             pltpu.SemaphoreType.DMA((devices,)),
         ]
-        + step_scratch(total, frames),
+        + step_scratch(total, frames)
+        + [pltpu.VMEM(array.shape, array.dtype) for array in (*weights, features)]
+        + [pltpu.SemaphoreType.DMA((4,))],
         compiler_params=pltpu.CompilerParams(
-            collective_id=2, has_side_effects=True, vmem_limit_bytes=40 << 20
+            collective_id=2, has_side_effects=True, vmem_limit_bytes=67043328
         ),
         name="fused_step",
     )(frame_lens, label_lens, features, labels, *weights)
@@ -639,7 +653,7 @@
         out_shape=shapes * 3,
         in_specs=[VMEM] * 13,
         out_specs=[VMEM] * 9,
-        compiler_params=pltpu.CompilerParams(vmem_limit_bytes=8 << 20),
+        compiler_params=pltpu.CompilerParams(vmem_limit_bytes=67043328),
         name="adam",
     )(squares, *weights, *firsts, *seconds, *grads)
 

time: 77.3 us -> 75.5 us (0.977)
  local copies, waits for them, and re-layouts: 3.17 us -> 0 us
  Pallas kernels: 73.1 us -> 74.6 us
    unnamed x26 -> x0, local copies, waits for them, and re-layouts: 3.17 us -> none
    pallas_call x1, Pallas kernels: 0.87 us -> 1.81 us  [adam(): pl.pallas_call(adam_kernel, out_shape=shapes * 3, in_specs=[VMEM] * 13, o...]
where the time goes in v3:
time: 75.5 us; the launch traced here: 75.2 us
  Pallas kernels  74.6 us (99%)
    pallas_call x1, Pallas kernels, fused_step(): pl.pallas_call(functools.partial(fused_kernel, devices, loss_scale), out_...  72.8 us
    pallas_call x1, Pallas kernels, adam(): pl.pallas_call(adam_kernel, out_shape=shapes * 3, in_specs=[VMEM] * 13, o...  1.81 us

profile of v3, /device:TPU:0, one launch (start us, length us, event | category | flops | bytes accessed | tf_op | source)
XLA Modules:
  0.0 75.2 jit_solution(152096052148345140)
XLA Ops:
  0.6 72.8 %fused_step.1 = (f32[64,128]{1,0:T(8,128)}, f32[64,128]{1,0:T(8,128)}, f32[16,128]{1,0:T(8,128)}, f32[32,1,128]{2,1,0:T(1,128)}) custom-call(s32[2]{0:T(128)} %refs_0_.1, s32[2]{0:T(128)} %refs_1_.1, bf16[512,256]{1,0:T(8,128)(2,1)} %bitcast.19, s32[2,48]{1,0:T(2,128)} %refs_3_.1, f32[64,128]{1,0:T(8,128)} %bitcast.20, f32[64,128]{1,0:T(8,128)} %bitcast.22, ...), custom_call_target="tpu_custom_call" | custom-call | tf_op jit(solution)/shard_map/fused_step/pallas_call | solution.py:580
  73.4 1.8 %adam.1 = (f32[64,128]{1,0:T(8,128)}, f32[64,128]{1,0:T(8,128)}, f32[16,128]{1,0:T(8,128)}, f32[64,128]{1,0:T(8,128)}, f32[64,128]{1,0:T(8,128)}, /*index=5*/f32...) custom-call(f32[32,1,128]{2,1,0:T(1,128)} %get-tuple-element.22.squares, f32[64,128]{1,0:T(8,128)} %bitcast.21, ...), custom_call_target="tpu_custom_call" | custom-call | tf_op jit(solution)/shard_map/adam/pallas_call | solution.py:651
